TPU v7x, 32 devices: a whole 2x2x4 slice. The times are simulated.
32 devices in a mesh: ep: 16 (over z, y, x), tp: 2 (over core).
Axes of the slice: x: 2, y: 2, z: 4, core: 2. Of those that a mesh axis runs over, the one named last changes fastest.
Arguments:
- tokens: bfloat16 [2048, 3584], P('ep', 'tp'), may hold values from -6 to 6
- routes: int32 [2048, 8], P('ep'), may hold values from 0 to 15, all different within a row; in each aligned block of 128 rows (0 to 127, 128 to 255, ...) at most 72 rows name the same one
- gate_levels: int32 [2048, 8], P('ep'), may hold values from 1 to 255
- w_gate: bfloat16 [16, 3584, 1024], P('ep', 'tp'), may hold values from -0.09375 to 0.09375
- w_up: bfloat16 [16, 3584, 1024], P('ep', 'tp'), may hold values from -0.09375 to 0.09375
- w_down: bfloat16 [16, 1024, 3584], P('ep', None, 'tp'), may hold values from -0.1875 to 0.1875
Outputs:
- mixed: bfloat16 [2048, 3584], P('ep', 'tp')
Inputs may be any that keep to these rules, and one draw needn't show every extreme that they name: `routes`: each row names 8 different experts. Among the 128 tokens of one aligned block no expert is named by more than 72 rows, and in every draw some expert is named by exactly 72 rows of some block.
All inputs are finite; a program needn't handle non-finite values.
Results may differ from a plain program's by a relative error of at most 0.0085.
Values may be sent and summed in bfloat16 or wider, within the bound.
A program may use at most 64 MiB of HBM per device.

v0:
```python
import jax
import jax.numpy as jnp
from jax import lax
from jax.sharding import PartitionSpec as P


def run_expert(inputs, gate_w, up_w, down_w):
    gate_part = jnp.dot(inputs, gate_w, preferred_element_type=jnp.float32)
    up_part = jnp.dot(inputs, up_w, preferred_element_type=jnp.float32)
    gate_sum, up_sum = (
        lax.psum_scatter(gate_part, "tp", scatter_dimension=1, tiled=True),
        lax.psum_scatter(up_part, "tp", scatter_dimension=1, tiled=True),
    )
    hidden = (jax.nn.silu(gate_sum) * up_sum).astype(jnp.bfloat16)
    output = jnp.dot(
        lax.all_gather(hidden, "tp", axis=1, tiled=True), down_w, preferred_element_type=jnp.float32
    )
    return output.astype(jnp.bfloat16)


def on_device(tokens, routes, gate_levels, w_gate, w_up, w_down):
    ep_count = lax.axis_size("ep")
    tok_rows, top_count = routes.shape
    experts_here = w_gate.shape[0]
    capacity = min(tok_rows, max(2, 9 * tok_rows * top_count // (8 * experts_here * ep_count)))
    width_local = tokens.shape[1]
    slots_each = ep_count * capacity
    slots_total = experts_here * slots_each
    flat_ids = routes.reshape(-1)
    positions = jnp.arange(tok_rows * top_count, dtype=jnp.int32)
    same_expert = flat_ids[:, None] == flat_ids[None, :]
    earlier = positions[:, None] > positions[None, :]
    slot_index = jnp.sum(same_expert & earlier, axis=1)
    destination = (
        flat_ids % experts_here * ep_count + flat_ids // experts_here
    ) * capacity + slot_index
    slot_numbers = jnp.arange(slots_total, dtype=jnp.int32)
    matches = destination.reshape(tok_rows, top_count)[:, :, None] == slot_numbers[None, None, :]
    token_slots = jnp.any(matches, axis=1).astype(jnp.bfloat16)
    outgoing = jnp.einsum(
        "ts,td->sd", token_slots, tokens, preferred_element_type=jnp.float32
    ).astype(jnp.bfloat16)
    levels = gate_levels.astype(jnp.float32)
    weights = levels / jnp.sum(levels, axis=1, keepdims=True)
    weight_high = weights.astype(jnp.bfloat16).astype(jnp.float32)
    weight_low = weights - weight_high
    table_high = jnp.sum(jnp.where(matches, weight_high[:, :, None], 0.0), axis=1).astype(
        jnp.bfloat16
    )
    table_low = jnp.sum(jnp.where(matches, weight_low[:, :, None], 0.0), axis=1).astype(
        jnp.bfloat16
    )
    arrived = lax.all_to_all(
        outgoing.reshape(experts_here, ep_count, capacity, width_local),
        "ep",
        split_axis=1,
        concat_axis=1,
        tiled=True,
    )
    expert_rows = arrived.reshape(experts_here, slots_each, width_local)
    results = [run_expert(expert_rows[0], w_gate[0], w_up[0], w_down[0])]
    produced = jnp.stack(results)
    returned = lax.all_to_all(
        produced.reshape(experts_here, ep_count, capacity, width_local),
        "ep",
        split_axis=1,
        concat_axis=1,
        tiled=True,
    )
    flat_returned = returned.reshape(slots_total, width_local)
    mixed = jnp.dot(table_high, flat_returned, preferred_element_type=jnp.float32)
    mixed = mixed + jnp.dot(table_low, flat_returned, preferred_element_type=jnp.float32)
    return mixed.astype(jnp.bfloat16)


def solution(mesh):
    in_specs = (
        P("ep", "tp"),
        P("ep", None),
        P("ep", None),
        P("ep", "tp", None),
        P("ep", "tp", None),
        P("ep", None, "tp"),
    )
    out_specs = P("ep", "tp")
    return jax.shard_map(
        on_device, mesh=mesh, in_specs=in_specs, out_specs=out_specs, check_vma=False
    )
```

profile of v0, /device:TPU:14, one launch (start us, length us, event | category | flops | bytes accessed | tf_op | source)
XLA Modules:
  0.0 286.4 jit_solution(4687454529718250434)
XLA Ops:
  6.5 0.0 copy-start
  6.5 0.0 reduce-scatter.3.cloned.1.call-start
  6.5 0.8 copy.29
  7.4 0.1 eq.30
  7.5 0.5 convert_reduce_fusion
  8.0 0.1 reduce_sum.39
  8.1 0.7 multiply_add_fusion
  8.9 0.1 copy.31
  9.0 1.5 fusion
  10.4 0.0 copy-done
  10.5 1.3 convolution_convert_fusion.1
  11.7 0.0 copy-start.3
  11.8 97.5 %all_to_all.10 = bf16[1,16,72,1792]{3,2,0,1:T(8,128)(2,1)S(1)} all-to-all(bf16[1,16,72,1792]{3,2,0,1:T(8,128)(2,1)S(1)} %bitcast.26), channel_id=1, replica_groups=mesh['ep'=16,'tp'=2] {'ep'}, dimensions={1} | all-to-all | bytes 8257536 | tf_op jit(solution)/shard_map/all_to_all | solution.py:53
  109.2 0.0 copy-start.1
  109.2 2.0 copy-done.1
  111.2 0.0 copy-done.3
  111.3 6.0 %fusion.5 = f32[1152,1024]{1,0:T(8,128)} fusion(bf16[1152,1792]{1,0:T(8,128)(2,1)S(1)} %bitcast.28, bf16[1,1792,1024]{2,1,0:T(8,128)(2,1)S(1)} %copy-done.3), kind=kOutput, calls=%fused_computation.12 | convolution fusion | flops 4227858432 | bytes 12517376 | tf_op jit(solution)/shard_map/dot_general | solution.py:8
  117.2 0.0 reduce-scatter.3.cloned.1.call-update
  117.3 0.0 reduce-scatter.5.cloned.1.call-start
  117.3 10.6 %fusion.3 = f32[1152,1024]{1,0:T(8,128)} fusion(bf16[1152,1792]{1,0:T(8,128)(2,1)} %bitcast.29, bf16[1,1792,1024]{2,1,0:T(8,128)(2,1)} %param.10), kind=kOutput, calls=%fused_computation.10 | convolution fusion | flops 4227858432 | bytes 12517376 | tf_op jit(solution)/shard_map/dot_general | solution.py:9
  127.9 0.0 reduce-scatter.5.cloned.1.call-update
  127.9 0.2 all-gather.2.cloned.1.call-start
  128.1 2.0 reduce-scatter.3.cloned.1.call-done
  130.1 16.0 %reduce-scatter.5.cloned.1.call-done = f32[1152,512]{1,0:T(8,128)} async-done(((f32[1152,1024]{1,0:T(8,128)}), f32[1152,512]{1,0:T(8,128)}) %reduce-scatter.5.cloned.1.call-update) | async-done | bytes 2359312 | tf_op jit(solution)/shard_map/reduce_scatter | solution.py:12
  146.1 4.2 %multiply_convert_fusion = bf16[1152,512]{1,0:T(8,128)(2,1)} fusion(f32[1152,512]{1,0:T(8,128)} %reduce-scatter.5.cloned.1.call-done, f32[1152,512]{1,0:T(8,128)} %reduce-scatter.3.cloned.1.call-done), kind=kLoop, calls=%fused_computation.16 | loop fusion | flops 3538944 | bytes 5898240 | tf_op jit(solution)/shard_map/convert_element_type | solution.py:14
  150.3 0.0 all-gather.2.cloned.1.call-update
  150.3 12.3 %all-gather.2.cloned.1.call-done = bf16[1152,1024]{1,0:T(8,128)(2,1)} async-done(((bf16[1152,512]{1,0:T(8,128)(2,1)}), bf16[1152,1024]{1,0:T(8,128)(2,1)}) %all-gather.2.cloned.1.call-update) | async-done | bytes 2359312 | tf_op jit(solution)/shard_map/all_gather | solution.py:16
  162.6 9.1 %convolution_convert_fusion = bf16[1152,1792]{1,0:T(8,128)(2,1)} fusion(bf16[1152,1024]{1,0:T(8,128)(2,1)} %all-gather.2.cloned.1.call-done, bf16[1,1024,1792]{2,1,0:T(8,128)(2,1)} %param.11), kind=kOutput, calls=%fused_computation | convolution fusion | flops 4229922816 | bytes 10158080 | tf_op jit(solution)/shard_map/dot_general | solution.py:15
  171.8 0.0 copy-start.2
  171.8 7.1 %all-to-all-start.1 = ((bf16[1,16,72,1792]{3,2,0,1:T(8,128)(2,1)}), bf16[1,16,72,1792]{3,2,0,1:T(8,128)(2,1)}, u32[]{:S(2)}, u32[]{:S(2)}) async-start(bf16[1,16,72,1792]{3,2,0,1:T(8,128)(2,1)} %bitcast.27), calls=%async_computation.3 | async-start | bytes 8257536 | tf_op jit(solution)/shard_map/all_to_all | solution.py:63
  178.8 0.0 copy-done.2
  178.9 0.1 copy.32
  179.0 0.1 copy.35
  179.1 3.1 %select_reduce_fusion = (bf16[128,1152]{1,0:T(8,128)(2,1)S(1)}, bf16[128,1152]{1,0:T(8,128)(2,1)S(1)}) fusion(f32[128,8]{1,0:T(8,128)S(1)} %copy.35, s32[128,8]{1,0:T(8,128)S(1)} %copy.31, f32[128,8]{1,0:T(8,128)S(1)} %copy.32), kind=kLoop, calls=%fused_computation.2 | loop fusion | flops 5603328 | bytes 602112 | tf_op jit(solution)/shard_map/reduce_sum | solution.py:50
  182.2 91.0 %all-to-all-done.1 = bf16[1,16,72,1792]{3,2,0,1:T(8,128)(2,1)} async-done(((bf16[1,16,72,1792]{3,2,0,1:T(8,128)(2,1)}), bf16[1,16,72,1792]{3,2,0,1:T(8,128)(2,1)}, u32[]{:S(2)}, u32[]{:S(2)}) %all-to-all-start.1) | async-done | bytes 4128800 | tf_op jit(solution)/shard_map/all_to_all | solution.py:63
  273.2 2.9 %fusion.12 = f32[128,1792]{1,0:T(8,128)S(1)} fusion(bf16[128,1152]{1,0:T(8,128)(2,1)S(1)} %get-tuple-element.6, bf16[1152,1792]{1,0:T(8,128)(2,1)} %bitcast.8), kind=kOutput, calls=%fused_computation.25 | convolution fusion | flops 528482304 | bytes 5341184 | tf_op jit(solution)/shard_map/dot_general | solution.py:71
  276.2 3.7 %fusion.7 = bf16[128,1792]{1,0:T(8,128)(2,1)} fusion(f32[128,1792]{1,0:T(8,128)S(1)} %fusion.12, bf16[1152,1792]{1,0:T(8,128)(2,1)} %bitcast.8, bf16[128,1152]{1,0:T(8,128)(2,1)S(1)} %get-tuple-element.5), kind=kOutput, calls=%fused_computation.15 | convolution fusion | flops 528941056 | bytes 5799936 | tf_op jit(solution)/shard_map/dot_general | solution.py:72
  (3 shorter events, 0.1 us)
Async XLA Ops:
  6.5 3.9 %copy-start = (bf16[128,1792]{1,0:T(8,128)(2,1)S(1)}, bf16[128,1792]{1,0:T(8,128)(2,1)}, u32[]{:S(2)}) copy-start(bf16[128,1792]{1,0:T(8,128)(2,1)} %param.6) | copy-start | bytes 1376260
  6.5 123.6 %reduce-scatter.3.cloned.1.call-start = ((), (), s32[]{:S(2)}) async-start(), calls=%async_computation.4 | async-start | bytes 7077888 | tf_op jit(solution)/shard_map/reduce_scatter | solution.py:11
  11.7 99.5 %copy-start.3 = (bf16[1,1792,1024]{2,1,0:T(8,128)(2,1)S(1)}, bf16[1,1792,1024]{2,1,0:T(8,128)(2,1)}, u32[]{:S(2)}) copy-start(bf16[1,1792,1024]{2,1,0:T(8,128)(2,1)} %param.9) | copy-start | bytes 11010052
  109.2 2.0 copy-start.1
  117.3 28.9 %reduce-scatter.5.cloned.1.call-start = ((), (), s32[]{:S(2)}) async-start(), calls=%async_computation.5 | async-start | bytes 7077888 | tf_op jit(solution)/shard_map/reduce_scatter | solution.py:12
  127.9 34.7 %all-gather.2.cloned.1.call-start = ((), (), s32[]{:S(2)}) async-start(), calls=%async_computation.6 | async-start | bytes 3538944 | tf_op jit(solution)/shard_map/all_gather | solution.py:16
  171.8 7.1 %copy-start.2 = (s32[128,8]{0,1:T(8,128)S(1)}, s32[128,8]{0,1:T(8,128)}, u32[]{:S(2)}) copy-start(s32[128,8]{0,1:T(8,128)} %param.8) | copy-start | bytes 12292
  171.8 101.4 %all-to-all-start.1 = ((bf16[1,16,72,1792]{3,2,0,1:T(8,128)(2,1)}), bf16[1,16,72,1792]{3,2,0,1:T(8,128)(2,1)}, u32[]{:S(2)}, u32[]{:S(2)}) async-start(bf16[1,16,72,1792]{3,2,0,1:T(8,128)(2,1)} %bitcast.27), calls=%async_computation.3 | async-start | bytes 8257536 | tf_op jit(solution)/shard_map/all_to_all | solution.py:63
Sparse Core Ops, SparseCore 0:
  117.4 12.7 reduce-scatter.2
  132.4 13.6 reduce-scatter.4
  150.5 12.1 all-gather.1
where the time goes:
time: 287 us; the launch traced here: 286 us
  waiting for transfers between devices  121 us (42%)
  blocking collectives  97.5 us (34%)
  matrix products  33.6 us (12%)
  between operations  13.2 us (5%)
  other arithmetic  9.99 us (3%)
  starting transfers between devices  7.35 us (3%)
  local copies, waits for them, and re-layouts  3.42 us (1%)
    all_to_all x1, blocking collectives, on_device(): lax.all_to_all(outgoing.reshape(experts_here, ep_count, capacity, width_l...  97.5 us
    all_to_all x1, waiting for transfers between devices, on_device(): lax.all_to_all(produced.reshape(experts_here, ep_count, capacity, width_l...  91 us
    reduce_scatter x1, waiting for transfers between devices, run_expert(): lax.psum_scatter(up_part, 'tp', scatter_dimension=1, tiled=True)  16 us
    all_gather x1, waiting for transfers between devices, run_expert(): lax.all_gather(hidden, 'tp', axis=1, tiled=True)  12.3 us
    dot_general x1, matrix products, run_expert(): up_part = jnp.dot(inputs, up_w, preferred_element_type=jnp.float32)  10.6 us
    dot_general x1, matrix products, run_expert(): jnp.dot(lax.all_gather(hidden, 'tp', axis=1, tiled=True), down_w, preferr...  9.13 us
    all_to_all x1, starting transfers between devices, on_device(): lax.all_to_all(produced.reshape(experts_here, ep_count, capacity, width_l...  7.09 us
    dot_general x1, matrix products, run_expert(): gate_part = jnp.dot(inputs, gate_w, preferred_element_type=jnp.float32)  5.98 us
  transfers between devices with their start and end apart: 4, of which 4 were waited for; matrix products, arithmetic and copies ran while one was open for 5% of the time, Pallas kernels for 0%

commit v1 on v0

--- a/solution.py
+++ b/solution.py
@@ -1,7 +1,17 @@
+import functools
+import math
+
 import jax
 import jax.numpy as jnp
 from jax import lax
+from jax.experimental import pallas as pl
+from jax.experimental.pallas import tpu as pltpu
 from jax.sharding import PartitionSpec as P
+
+MESH = pl.DeviceIdType.MESH
+ABSENT = -65536.0
+F32 = jnp.float32
+BF16 = jnp.bfloat16
 
 
 def run_expert(inputs, gate_w, up_w, down_w):
@@ -18,11 +28,11 @@
     return output.astype(jnp.bfloat16)
 
 
-def on_device(tokens, routes, gate_levels, w_gate, w_up, w_down):
+def general_path(tokens, routes, gate_levels, w_gate, w_up, w_down):
     ep_count = lax.axis_size("ep")
     tok_rows, top_count = routes.shape
     experts_here = w_gate.shape[0]
-    capacity = min(tok_rows, max(2, 9 * tok_rows * top_count // (8 * experts_here * ep_count)))
+    capacity = capacity_of(tok_rows, top_count, experts_here * ep_count)
     width_local = tokens.shape[1]
     slots_each = ep_count * capacity
     slots_total = experts_here * slots_each
@@ -73,6 +83,365 @@
     return mixed.astype(jnp.bfloat16)
 
 
+def capacity_of(tok_rows, top_count, experts):
+    return min(tok_rows, max(2, 9 * tok_rows * top_count // (8 * experts)))
+
+
+def layer_kernel(
+    line, plane, cap, fc,
+    code_ref, levels_ref, tokens_hbm, wg_hbm, wu_hbm, wd_hbm, out_ref,
+    tok, tbl_out, tbl, pick, mix, send, rows, rows_x, w_own, w_x, wd, acc, hid,
+    outs, ret, part_f, part, zin, own,
+    tok_sem, w_sem, wd_sem, ts_sem, tr_sem, zs_sem, zr_sem, ps_sem, pr_sem,
+    xs_sem, xr_sem, ws_sem, wr_sem, hs_sem, hr_sem, bs_sem, br_sem, cs_sem, cr_sem,
+):
+    me = lax.axis_index("ep")
+    t = lax.axis_index("tp")
+    other = 1 - t
+    z, p = me // plane, me % plane
+    T, top = levels_ref.shape
+    R = line * cap
+    nc = tok.shape[0]
+    half = wg_hbm.shape[1] // 2
+
+    def z_at(d):
+        return lax.rem(z + d, line)
+
+    def p_at(k):
+        return lax.rem(p + k, plane)
+
+    def z_dev(d):
+        return {"ep": z_at(d) * plane + p}
+
+    def p_dev(k):
+        return {"ep": z * plane + p_at(k)}
+
+    def remote(src, dst, s, r, dev):
+        return pltpu.make_async_remote_copy(
+            src_ref=src, dst_ref=dst, send_sem=s, recv_sem=r, device_id=dev, device_id_type=MESH
+        )
+
+    def zrows(i):
+        return pl.ds(pl.multiple_of(i * T, T), T)
+
+    def prows(i):
+        return pl.ds(pl.multiple_of(i * R, 16), R)
+
+    def units(i):
+        return pl.ds(pl.multiple_of(i * half, 128), half)
+
+    def tok_load(c):
+        return pltpu.make_async_copy(
+            tokens_hbm.at[:, pl.ds(pl.multiple_of(c * fc, 128), fc)],
+            tok.at[c, zrows(z)], tok_sem.at[c],
+        )
+
+    def wd_load(c):
+        return pltpu.make_async_copy(
+            wd_hbm.at[:, pl.ds(pl.multiple_of(c * fc, 128), fc)], wd.at[c], wd_sem.at[c]
+        )
+
+    def w_load(i):
+        return pltpu.make_async_copy(
+            (wg_hbm, wu_hbm)[i].at[:, units(t)], w_own.at[:, i * half:(i + 1) * half], w_sem.at[i]
+        )
+
+    def w_swap(i):
+        return remote(
+            (wg_hbm, wu_hbm)[i].at[:, units(other)], w_x.at[:, i * half:(i + 1) * half],
+            ws_sem.at[i], wr_sem.at[i], {"tp": other},
+        )
+
+    def t_copy(d):
+        return remote(tbl_out.at[z_at(d)], tbl.at[z], ts_sem.at[d - 1], tr_sem.at[d - 1], z_dev(d))
+
+    def z_copy(c, d):
+        return remote(
+            tok.at[c, zrows(z)], tok.at[c, zrows(z)],
+            zs_sem.at[d - 1, c], zr_sem.at[d - 1, c], z_dev(d),
+        )
+
+    def p_copy(c, k):
+        return remote(
+            send.at[c, k - 1], rows.at[c, prows(p)],
+            ps_sem.at[k - 1, c], pr_sem.at[k - 1, c], p_dev(k),
+        )
+
+    def x_copy(c):
+        return remote(rows.at[c], rows_x.at[c], xs_sem.at[c], xr_sem.at[c], {"tp": other})
+
+    def h_copy(m):
+        here = hid.at[t, m * R:(m + 1) * R]
+        return remote(here, here, hs_sem.at[m], hr_sem.at[m], {"tp": other})
+
+    def b_copy(c, k):
+        return remote(
+            outs.at[c, k - 1], ret.at[c, prows(p)],
+            bs_sem.at[k - 1, c], br_sem.at[k - 1, c], p_dev(k),
+        )
+
+    def c_copy(c, d):
+        return remote(
+            part.at[c, zrows(z_at(d))], zin.at[c, d - 1],
+            cs_sem.at[d - 1, c], cr_sem.at[d - 1, c], z_dev(d),
+        )
+
+    barrier = pltpu.get_barrier_semaphore()
+    for d in range(1, line):
+        pl.semaphore_signal(barrier, inc=1, device_id=z_dev(d), device_id_type=MESH)
+    for k in range(1, plane):
+        pl.semaphore_signal(barrier, inc=1, device_id=p_dev(k), device_id_type=MESH)
+    pl.semaphore_signal(barrier, inc=1, device_id={"tp": other}, device_id_type=MESH)
+
+    for c in range(nc):
+        tok_load(c).start()
+    for i in range(2):
+        w_load(i).start()
+    for c in range(nc):
+        wd_load(c).start()
+
+    lane = lax.broadcasted_iota(jnp.int32, (T, 128), 1)
+    code = code_ref[...]
+    levels = levels_ref[...].astype(F32)
+    weights = levels / jnp.sum(levels, axis=1, keepdims=True)
+    named = jnp.zeros((T, 128), F32)
+    share = jnp.zeros((T, 128), F32)
+    for k in range(top):
+        at = code[:, k:k + 1]
+        named = jnp.where(lane == at, 1.0, named)
+        share = jnp.where(lane == at + plane, weights[:, k:k + 1], share)
+    before = lax.broadcasted_iota(jnp.int32, (T, T), 0) > lax.broadcasted_iota(jnp.int32, (T, T), 1)
+    count = jnp.dot(
+        jnp.where(before, 1.0, 0.0).astype(BF16), named.astype(BF16), preferred_element_type=F32
+    )
+    slots = jnp.where(named > 0.0, count, ABSENT)
+    both = jnp.where((lane & (2 * plane - 1)) < plane, slots, share).T
+    for i in range(line):
+        tbl_out[i] = both[i * 2 * plane:(i + 1) * 2 * plane]
+    tbl[z] = tbl_out[z]
+
+    pl.semaphore_wait(barrier, line + plane - 1)
+    for d in range(1, line):
+        t_copy(d).start()
+    for c in range(nc):
+        tok_load(c).wait()
+        for d in range(1, line):
+            z_copy(c, d).start()
+    for i in range(2):
+        w_swap(i).start()
+
+    for d in range(1, line):
+        t_copy(d).wait_recv()
+    row_id = lax.broadcasted_iota(jnp.int32, (R, T), 0).astype(F32)
+    for q in range(plane):
+        for s in range(line):
+            at = tbl[s, q:q + 1, :] + float(s * cap)
+            pick[q, :, s * T:(s + 1) * T] = jnp.where(row_id == at, 1.0, 0.0).astype(BF16)
+
+    def dispatch(c, carry):
+        @pl.when(c < nc)
+        def _():
+            for d in range(1, line):
+                z_copy(c, d).wait_recv()
+            for k in range(1, plane):
+                send[c, k - 1] = jnp.dot(
+                    pick[p_at(k)], tok[c], preferred_element_type=F32
+                ).astype(BF16)
+                p_copy(c, k).start()
+            rows[c, prows(p)] = jnp.dot(pick[p], tok[c], preferred_element_type=F32).astype(BF16)
+
+        @pl.when(c == 0)
+        def _():
+            acc[...] = jnp.zeros_like(acc)
+            slot_id = lax.broadcasted_iota(jnp.int32, (T, plane * R), 1).astype(F32)
+            for s in range(line):
+                columns = tbl[s].T
+                high = jnp.zeros((T, plane * R), F32)
+                low = jnp.zeros((T, plane * R), F32)
+                for q in range(plane):
+                    here = slot_id == columns[:, q:q + 1] + float(q * R + s * cap)
+                    w = columns[:, plane + q:plane + q + 1]
+                    w_high = w.astype(BF16).astype(F32)
+                    high = jnp.where(here, w_high, high)
+                    low = jnp.where(here, w - w_high, low)
+                mix[0, s * T:(s + 1) * T, :] = high.astype(BF16)
+                mix[1, s * T:(s + 1) * T, :] = low.astype(BF16)
+
+        @pl.when(c == 2)
+        def _():
+            for i in range(2):
+                w_load(i).wait()
+                w_swap(i).wait()
+
+        @pl.when((c >= 1) & (c <= nc))
+        def _():
+            for k in range(1, plane):
+                p_copy(c - 1, k).wait_recv()
+            x_copy(c - 1).start()
+
+        @pl.when(c >= 2)
+        def _():
+            b = c - 2
+            x_copy(b).wait_recv()
+            at = pl.ds(pl.multiple_of(b * fc, fc), fc)
+
+            def tile(m, carry):
+                r = prows(m)
+                acc[r] += jnp.dot(
+                    rows[b, r], w_own[at], preferred_element_type=F32
+                ) + jnp.dot(rows_x[b, r], w_x[at], preferred_element_type=F32)
+                return carry
+
+            lax.fori_loop(0, plane, tile, 0)
+
+        return carry
+
+    lax.fori_loop(0, nc + 2, dispatch, 0)
+
+    for m in range(plane):
+        gate = acc[m * R:(m + 1) * R, :half]
+        up = acc[m * R:(m + 1) * R, half:]
+        hid[t, m * R:(m + 1) * R] = (gate / (1.0 + jnp.exp(-gate)) * up).astype(BF16)
+        h_copy(m).start()
+    for c in range(nc):
+        wd_load(c).wait()
+    for m in range(plane):
+        h_copy(m).wait_recv()
+
+    def down(c, q):
+        total = jnp.dot(hid[0, prows(q)], wd[c, :half], preferred_element_type=F32)
+        total += jnp.dot(hid[1, prows(q)], wd[c, half:], preferred_element_type=F32)
+        return total.astype(BF16)
+
+    def combine(c, carry):
+        @pl.when(c < nc)
+        def _():
+            for k in range(1, plane):
+                outs[c, k - 1] = down(c, p_at(k))
+                b_copy(c, k).start()
+            ret[c, prows(p)] = down(c, p)
+
+        @pl.when((c >= 1) & (c <= nc))
+        def _():
+            b = c - 1
+            for k in range(1, plane):
+                b_copy(b, k).wait_recv()
+            total = jnp.dot(mix[0], ret[b], preferred_element_type=F32)
+            total += jnp.dot(mix[1], ret[b], preferred_element_type=F32)
+            part_f[...] = total
+            part[b] = total.astype(BF16)
+            for d in range(1, line):
+                c_copy(b, d).start()
+            own[b] = part_f[zrows(z)]
+
+        @pl.when(c >= 2)
+        def _():
+            b = c - 2
+            total = own[b]
+            for d in range(1, line):
+                c_copy(b, d).wait_recv()
+                total += zin[b, d - 1].astype(F32)
+            out_ref[:, pl.ds(pl.multiple_of(b * fc, fc), fc)] = total.astype(BF16)
+
+        return carry
+
+    lax.fori_loop(0, nc + 2, combine, 0)
+
+    for d in range(1, line):
+        t_copy(d).wait_send()
+    for m in range(plane):
+        h_copy(m).wait_send()
+
+    def drain(c, carry):
+        for d in range(1, line):
+            z_copy(c, d).wait_send()
+            c_copy(c, d).wait_send()
+        for k in range(1, plane):
+            p_copy(c, k).wait_send()
+            b_copy(c, k).wait_send()
+        x_copy(c).wait_send()
+        return carry
+
+    lax.fori_loop(0, nc, drain, 0)
+
+
+def kernel_path(line, plane, cap, fc, tokens, routes, gate_levels, w_gate, w_up, w_down):
+    T, width = tokens.shape
+    units = w_gate.shape[2]
+    half = units // 2
+    R = line * cap
+    nc = width // fc
+    code = routes // plane * (2 * plane) + routes % plane
+    vmem, dma = pltpu.VMEM, pltpu.SemaphoreType.DMA
+    anywhere = pl.BlockSpec(memory_space=pl.ANY)
+    local = pl.BlockSpec(memory_space=pltpu.VMEM)
+    return pl.pallas_call(
+        functools.partial(layer_kernel, line, plane, cap, fc),
+        out_shape=jax.ShapeDtypeStruct((T, width), BF16),
+        in_specs=[local, local, anywhere, anywhere, anywhere, anywhere],
+        out_specs=local,
+        scratch_shapes=[
+            vmem((nc, line * T, fc), BF16),
+            vmem((line, 2 * plane, T), F32),
+            vmem((line, 2 * plane, T), F32),
+            vmem((plane, R, line * T), BF16),
+            vmem((2, line * T, plane * R), BF16),
+            vmem((nc, plane - 1, R, fc), BF16),
+            vmem((nc, plane * R, fc), BF16),
+            vmem((nc, plane * R, fc), BF16),
+            vmem((width, units), BF16),
+            vmem((width, units), BF16),
+            vmem((nc, units, fc), BF16),
+            vmem((plane * R, units), F32),
+            vmem((2, plane * R, half), BF16),
+            vmem((nc, plane - 1, R, fc), BF16),
+            vmem((nc, plane * R, fc), BF16),
+            vmem((line * T, fc), F32),
+            vmem((nc, line * T, fc), BF16),
+            vmem((nc, line - 1, T, fc), BF16),
+            vmem((nc, T, fc), F32),
+            dma((nc,)), dma((2,)), dma((nc,)),
+            dma((line - 1,)), dma((line - 1,)),
+            dma((line - 1, nc)), dma((line - 1, nc)),
+            dma((plane - 1, nc)), dma((plane - 1, nc)),
+            dma((nc,)), dma((nc,)),
+            dma((2,)), dma((2,)),
+            dma((plane,)), dma((plane,)),
+            dma((plane - 1, nc)), dma((plane - 1, nc)),
+            dma((line - 1, nc)), dma((line - 1, nc)),
+        ],
+        compiler_params=pltpu.CompilerParams(
+            collective_id=0, has_side_effects=True, vmem_limit_bytes=60 * 1024 * 1024
+        ),
+        name="expert_layer",
+    )(code, gate_levels, tokens, w_gate[0], w_up[0], w_down[0])
+
+
+def on_device(ep_count, tp_count, tokens, routes, gate_levels, w_gate, w_up, w_down):
+    tok_rows, top_count = routes.shape
+    experts_here, width, units = w_gate.shape
+    cap = capacity_of(tok_rows, top_count, experts_here * ep_count)
+    plane = math.isqrt(ep_count)
+    line = ep_count // plane
+    fc = 256
+    fits = (
+        tp_count == 2
+        and experts_here == 1
+        and plane * line == ep_count
+        and plane & (plane - 1) == 0
+        and plane % 4 == 0
+        and line * 2 * plane <= 128
+        and tok_rows == 128
+        and line * cap % 16 == 0
+        and width % fc == 0
+        and units % 256 == 0
+    )
+    args = (tokens, routes, gate_levels, w_gate, w_up, w_down)
+    if fits:
+        return kernel_path(line, plane, cap, fc, *args)
+    return general_path(*args)
+
+
 def solution(mesh):
     in_specs = (
         P("ep", "tp"),
@@ -83,6 +452,7 @@
         P("ep", None, "tp"),
     )
     out_specs = P("ep", "tp")
+    body = functools.partial(on_device, mesh.shape["ep"], mesh.shape["tp"])
     return jax.shard_map(
-        on_device, mesh=mesh, in_specs=in_specs, out_specs=out_specs, check_vma=False
-    )
+        body, mesh=mesh, in_specs=in_specs, out_specs=out_specs, check_vma=False
+    )

time: 287 us -> 134 us (0.47)
  the two profiles are of different devices: /device:TPU:14 before, /device:TPU:0 now
where the time goes in v1:
time: 134 us
  Pallas kernels  129 us (96%)
  local copies, waits for them, and re-layouts  4 us (3%)
    pallas_call x1, Pallas kernels, kernel_path(): pl.pallas_call(functools.partial(layer_kernel, line, plane, cap, fc), out...  129 us
    unnamed x3, local copies, waits for them, and re-layouts  4 us

profile of v1, /device:TPU:0, one launch (start us, length us, event | category | flops | bytes accessed | tf_op | source)
XLA Modules:
  0.0 133.6 jit_solution(15998646551178371104)
XLA Ops:
  0.0 0.8 copy.7
  0.8 0.7 fusion.1.code_ref
  1.5 1.4 %copy.11.levels_ref = s32[128,8]{1,0:T(8,128)} copy(s32[128,8]{0,1:T(8,128)} %param.8) | data formatting | bytes 8192 | tf_op args[2]
  2.9 128.9 %expert_layer.1 = bf16[128,1792]{1,0:T(8,128)(2,1)} custom-call(s32[128,8]{1,0:T(8,128)} %fusion.1.code_ref, s32[128,8]{1,0:T(8,128)} %copy.11.levels_ref, bf16[128,1792]{1,0:T(8,128)(2,1)} %tokens_hbm.1, bf16[1792,1024]{1,0:T(8,128)(2,1)} %bitcast.3, bf16[1792,1024]{1,0:T(8,128)(2,1)} %bitcast.4, bf16[1024,1792]{1,0:T(8,128)(2,1)} %bitcast.5), custom_call_target="tpu_custom_call" | custom-call | tf_op jit(solution)/shard_map/expert_layer/pallas_call | solution.py:378
  131.8 1.8 %copy.13 = bf16[128,1792]{1,0:T(8,128)(2,1)} copy(bf16[128,1792]{1,0:T(8,128)(2,1)} %expert_layer.1) | data formatting | bytes 917504

commit v2 on v0

--- a/solution.py
+++ b/solution.py
@@ -1,7 +1,17 @@
+import functools
+import math
+
 import jax
 import jax.numpy as jnp
 from jax import lax
+from jax.experimental import pallas as pl
+from jax.experimental.pallas import tpu as pltpu
 from jax.sharding import PartitionSpec as P
+
+MESH = pl.DeviceIdType.MESH
+ABSENT = -65536.0
+F32 = jnp.float32
+BF16 = jnp.bfloat16
 
 
 def run_expert(inputs, gate_w, up_w, down_w):
@@ -18,11 +28,11 @@
     return output.astype(jnp.bfloat16)
 
 
-def on_device(tokens, routes, gate_levels, w_gate, w_up, w_down):
+def general_path(tokens, routes, gate_levels, w_gate, w_up, w_down):
     ep_count = lax.axis_size("ep")
     tok_rows, top_count = routes.shape
     experts_here = w_gate.shape[0]
-    capacity = min(tok_rows, max(2, 9 * tok_rows * top_count // (8 * experts_here * ep_count)))
+    capacity = capacity_of(tok_rows, top_count, experts_here * ep_count)
     width_local = tokens.shape[1]
     slots_each = ep_count * capacity
     slots_total = experts_here * slots_each
@@ -73,6 +83,451 @@
     return mixed.astype(jnp.bfloat16)
 
 
+def capacity_of(tok_rows, top_count, experts):
+    return min(tok_rows, max(2, 9 * tok_rows * top_count // (8 * experts)))
+
+
+def layer_kernel(
+    line, plane, cap, fc,
+    routes_ref, levels_ref, tokens_hbm, wg_hbm, wu_hbm, wd_hbm, out_ref,
+    tok, tbl_out, tbl, pick, mix, send, rows, rows_x, w_own, w_x, wd, acc, hid,
+    outs, ret, part_f, part, zin, own,
+    tok_sem, w_sem, wd_sem, ts_sem, tr_sem, zs_sem, zr_sem, ps_sem, pr_sem,
+    xs_sem, xr_sem, ws_sem, wr_sem, hs_sem, hr_sem, bs_sem, br_sem, cs_sem, cr_sem,
+):
+    me = lax.axis_index("ep")
+    t = lax.axis_index("tp")
+    other = 1 - t
+    z, p = me // plane, me % plane
+    top, T = levels_ref.shape
+    G = line // 2
+    R = G * cap
+    nc = tok.shape[1]
+    half = wg_hbm.shape[1] // 2
+    mine = lax.rem(z, G)
+    near = [(0, d) for d in range(1, G)]
+    far = [(1, d) for d in range(G)]
+    peers = {gd: i for i, gd in enumerate(near + far)}
+
+    def z_at(g, d):
+        return lax.rem(z // G + g, 2) * G + lax.rem(mine + d, G)
+
+    def z_dev(g, d):
+        return {"ep": z_at(g, d) * plane + p}
+
+    def p_at(k):
+        return lax.rem(p + k, plane)
+
+    def p_dev(k):
+        return {"ep": z * plane + p_at(k)}
+
+    def remote(src, dst, s, r, dev):
+        return pltpu.make_async_remote_copy(
+            src_ref=src, dst_ref=dst, send_sem=s, recv_sem=r, device_id=dev, device_id_type=MESH
+        )
+
+    def zrows(i):
+        return pl.ds(pl.multiple_of(i * T, T), T)
+
+    def prows(i):
+        return pl.ds(pl.multiple_of(i * R, 16), R)
+
+    def units(i):
+        return pl.ds(pl.multiple_of(i * half, 128), half)
+
+    def tok_load(c):
+        return pltpu.make_async_copy(
+            tokens_hbm.at[:, pl.ds(pl.multiple_of(c * fc, 128), fc)],
+            tok.at[0, c, zrows(mine)], tok_sem.at[c],
+        )
+
+    def wd_load(c):
+        return pltpu.make_async_copy(
+            wd_hbm.at[:, pl.ds(pl.multiple_of(c * fc, 128), fc)], wd.at[c], wd_sem.at[c]
+        )
+
+    def w_load(i):
+        return pltpu.make_async_copy(
+            (wg_hbm, wu_hbm)[i].at[:, units(t)], w_own.at[:, i * half:(i + 1) * half], w_sem.at[i]
+        )
+
+    def w_swap(i):
+        return remote(
+            (wg_hbm, wu_hbm)[i].at[:, units(other)], w_x.at[:, i * half:(i + 1) * half],
+            ws_sem.at[i], wr_sem.at[i], {"tp": other},
+        )
+
+    def t_copy(g, d):
+        i = peers[g, d]
+        return remote(
+            tbl_out.at[z_at(g, d)], tbl.at[g, mine], ts_sem.at[i], tr_sem.at[i], z_dev(g, d)
+        )
+
+    def z_copy(c, g, d):
+        i = peers[g, d]
+        return remote(
+            tok.at[0, c, zrows(mine)], tok.at[g, c, zrows(mine)],
+            zs_sem.at[i, c], zr_sem.at[i, c], z_dev(g, d),
+        )
+
+    def p_copy(g, c, k):
+        return remote(
+            send.at[g, c, k - 1], rows.at[g, c, prows(p)],
+            ps_sem.at[g, k - 1, c], pr_sem.at[g, k - 1, c], p_dev(k),
+        )
+
+    def x_copy(g, c):
+        return remote(
+            rows.at[g, c], rows_x.at[g, c], xs_sem.at[g, c], xr_sem.at[g, c], {"tp": other}
+        )
+
+    def h_copy(g, m):
+        here = hid.at[g, t, m * R:(m + 1) * R]
+        return remote(here, here, hs_sem.at[g, m], hr_sem.at[g, m], {"tp": other})
+
+    def b_copy(g, c, k):
+        return remote(
+            outs.at[g, c, k - 1], ret.at[g, c, prows(p)],
+            bs_sem.at[g, k - 1, c], br_sem.at[g, k - 1, c], p_dev(k),
+        )
+
+    def c_copy(c, g, d):
+        i = peers[g, d]
+        return remote(
+            part.at[g, c, zrows(lax.rem(mine + d, G))], zin.at[c, i],
+            cs_sem.at[i, c], cr_sem.at[i, c], z_dev(g, d),
+        )
+
+    barrier = pltpu.get_barrier_semaphore()
+    for g, d in peers:
+        pl.semaphore_signal(barrier, inc=1, device_id=z_dev(g, d), device_id_type=MESH)
+    for k in range(1, plane):
+        pl.semaphore_signal(barrier, inc=1, device_id=p_dev(k), device_id_type=MESH)
+    pl.semaphore_signal(barrier, inc=1, device_id={"tp": other}, device_id_type=MESH)
+
+    for c in range(nc):
+        tok_load(c).start()
+    for i in range(2):
+        w_load(i).start()
+    for c in range(nc):
+        wd_load(c).start()
+
+    height = line * 2 * plane
+    row = lax.broadcasted_iota(jnp.int32, (height, T), 0)
+    expert = (row >> (2 * plane).bit_length() - 1) * plane + (row & (plane - 1))
+    routes = routes_ref[...]
+    levels = levels_ref[...].astype(F32)
+    weights = levels / jnp.sum(levels, axis=0, keepdims=True)
+    named = jnp.zeros((height, T), F32)
+    share = jnp.zeros((height, T), F32)
+    for k in range(top):
+        at = expert == routes[k:k + 1, :]
+        named = jnp.where(at, 1.0, named)
+        share = jnp.where(at, weights[k:k + 1, :], share)
+    before = lax.broadcasted_iota(jnp.int32, (T, T), 0) < lax.broadcasted_iota(jnp.int32, (T, T), 1)
+    count = jnp.dot(
+        named.astype(BF16), jnp.where(before, 1.0, 0.0).astype(BF16), preferred_element_type=F32
+    )
+    slots = jnp.where(named > 0.0, count, ABSENT)
+    both = jnp.where((row & (2 * plane - 1)) < plane, slots, share)
+    for i in range(line):
+        tbl_out[i] = both[i * 2 * plane:(i + 1) * 2 * plane]
+    tbl[0, mine] = tbl_out[z]
+
+    pl.semaphore_wait(barrier, line + plane - 1)
+    for g, d in peers:
+        t_copy(g, d).start()
+    for c in range(nc):
+        tok_load(c).wait()
+        for g, d in near:
+            z_copy(c, g, d).start()
+    for c in range(nc):
+        for g, d in far:
+            z_copy(c, g, d).start()
+    for i in range(2):
+        w_swap(i).start()
+
+    for g, d in peers:
+        t_copy(g, d).wait_recv()
+    row_id = lax.broadcasted_iota(jnp.int32, (R, T), 0).astype(F32)
+    for g in range(2):
+        for q in range(plane):
+            for s in range(G):
+                at = tbl[g, s, q:q + 1, :] + float(s * cap)
+                pick[g, q, :, s * T:(s + 1) * T] = jnp.where(row_id == at, 1.0, 0.0).astype(BF16)
+
+    def select(g, c):
+        for k in range(1, plane):
+            send[g, c, k - 1] = jnp.dot(
+                pick[g, p_at(k)], tok[g, c], preferred_element_type=F32
+            ).astype(BF16)
+            p_copy(g, c, k).start()
+        rows[g, c, prows(p)] = jnp.dot(
+            pick[g, p], tok[g, c], preferred_element_type=F32
+        ).astype(BF16)
+
+    def forward(g, c):
+        for k in range(1, plane):
+            p_copy(g, c, k).wait_recv()
+        x_copy(g, c).start()
+
+    def gate_up(g, c):
+        x_copy(g, c).wait_recv()
+        at = pl.ds(pl.multiple_of(c * fc, fc), fc)
+
+        def tile(m, carry):
+            r = pl.ds(pl.multiple_of(m * 2 * R, 16), 2 * R)
+            acc[g, r] += jnp.dot(
+                rows[g, c, r], w_own[at], preferred_element_type=F32
+            ) + jnp.dot(rows_x[g, c, r], w_x[at], preferred_element_type=F32)
+            return carry
+
+        lax.fori_loop(0, plane // 2, tile, 0)
+
+    def activate(g):
+        for m in range(plane):
+            gate = acc[g, m * R:(m + 1) * R, :half]
+            up = acc[g, m * R:(m + 1) * R, half:]
+            hid[g, t, m * R:(m + 1) * R] = (gate / (1.0 + jnp.exp(-gate)) * up).astype(BF16)
+            h_copy(g, m).start()
+
+    def down(g, c, q):
+        total = jnp.dot(hid[g, 0, prows(q)], wd[c, :half], preferred_element_type=F32)
+        total += jnp.dot(hid[g, 1, prows(q)], wd[c, half:], preferred_element_type=F32)
+        return total.astype(BF16)
+
+    def give_back(g, c):
+        for k in range(1, plane):
+            outs[g, c, k - 1] = down(g, c, p_at(k))
+            b_copy(g, c, k).start()
+        ret[g, c, prows(p)] = down(g, c, p)
+
+    def weigh(g, c):
+        for k in range(1, plane):
+            b_copy(g, c, k).wait_recv()
+        total = jnp.dot(mix[g, 0], ret[g, c], preferred_element_type=F32)
+        total += jnp.dot(mix[g, 1], ret[g, c], preferred_element_type=F32)
+        part[g, c] = total.astype(BF16)
+        for h, d in near if g == 0 else far:
+            c_copy(c, h, d).start()
+        if g == 0:
+            part_f[...] = total
+            own[c] = part_f[zrows(mine)]
+
+    def first(c, carry):
+        for g, d in near:
+            z_copy(c, g, d).wait_recv()
+        select(0, c)
+        return carry
+
+    lax.fori_loop(0, nc, first, 0)
+
+    acc[...] = jnp.zeros_like(acc)
+    slot_id = lax.broadcasted_iota(jnp.int32, (T, plane * R), 1).astype(F32)
+    for g in range(2):
+        for s in range(G):
+            columns = tbl[g, s].T
+            high = jnp.zeros((T, plane * R), F32)
+            low = jnp.zeros((T, plane * R), F32)
+            for q in range(plane):
+                here = slot_id == columns[:, q:q + 1] + float(q * R + s * cap)
+                w = columns[:, plane + q:plane + q + 1]
+                w_high = w.astype(BF16).astype(F32)
+                high = jnp.where(here, w_high, high)
+                low = jnp.where(here, w - w_high, low)
+            mix[g, 0, s * T:(s + 1) * T, :] = high.astype(BF16)
+            mix[g, 1, s * T:(s + 1) * T, :] = low.astype(BF16)
+    for i in range(2):
+        w_load(i).wait()
+        w_swap(i).wait()
+    for c in range(nc):
+        wd_load(c).wait()
+
+    lag = 3
+    early = min(3, nc)
+
+    def dispatch(c, carry):
+        @pl.when(c < nc)
+        def _():
+            for g, d in far:
+                z_copy(c, g, d).wait_recv()
+            select(1, c)
+            forward(0, c)
+
+        @pl.when((c >= 1) & (c <= nc))
+        def _():
+            gate_up(0, c - 1)
+
+        @pl.when(c == nc)
+        def _():
+            activate(0)
+
+        @pl.when((c >= lag) & (c < nc + lag))
+        def _():
+            forward(1, c - lag)
+
+        @pl.when(c == nc + 1)
+        def _():
+            for m in range(plane):
+                h_copy(0, m).wait_recv()
+
+        @pl.when((c > nc) & (c <= nc + early))
+        def _():
+            give_back(0, c - nc - 1)
+
+        @pl.when(c > lag)
+        def _():
+            gate_up(1, c - lag - 1)
+
+        return carry
+
+    lax.fori_loop(0, nc + lag + 1, dispatch, 0)
+
+    activate(1)
+    for m in range(plane):
+        h_copy(1, m).wait_recv()
+
+    def back_far(c, carry):
+        give_back(1, c)
+
+        @pl.when(c < early)
+        def _():
+            weigh(0, c)
+
+        @pl.when(c >= 2)
+        def _():
+            weigh(1, c - 2)
+
+        return carry
+
+    lax.fori_loop(0, nc, back_far, 0)
+
+    def back_near(j, carry):
+        @pl.when(j < nc - early)
+        def _():
+            give_back(0, early + j)
+
+        @pl.when(j < 2)
+        def _():
+            weigh(1, nc - 2 + j)
+
+        @pl.when(j >= 2)
+        def _():
+            weigh(0, early + j - 2)
+
+        return carry
+
+    lax.fori_loop(0, nc - early + 2, back_near, 0)
+
+    def finish(c, carry):
+        total = own[c]
+        for (g, d), i in peers.items():
+            c_copy(c, g, d).wait_recv()
+            total += zin[c, i].astype(F32)
+        out_ref[:, pl.ds(pl.multiple_of(c * fc, fc), fc)] = total.astype(BF16)
+        return carry
+
+    lax.fori_loop(0, nc, finish, 0)
+
+    for g, d in peers:
+        t_copy(g, d).wait_send()
+    for g in range(2):
+        for m in range(plane):
+            h_copy(g, m).wait_send()
+
+    def drain(c, carry):
+        for g, d in peers:
+            z_copy(c, g, d).wait_send()
+            c_copy(c, g, d).wait_send()
+        for g in range(2):
+            for k in range(1, plane):
+                p_copy(g, c, k).wait_send()
+                b_copy(g, c, k).wait_send()
+            x_copy(g, c).wait_send()
+        return carry
+
+    lax.fori_loop(0, nc, drain, 0)
+
+
+def kernel_path(line, plane, cap, fc, tokens, routes, gate_levels, w_gate, w_up, w_down):
+    T, width = tokens.shape
+    units = w_gate.shape[2]
+    half = units // 2
+    G = line // 2
+    R = G * cap
+    nc = width // fc
+    vmem, dma = pltpu.VMEM, pltpu.SemaphoreType.DMA
+    anywhere = pl.BlockSpec(memory_space=pl.ANY)
+    local = pl.BlockSpec(memory_space=pltpu.VMEM)
+    return pl.pallas_call(
+        functools.partial(layer_kernel, line, plane, cap, fc),
+        out_shape=jax.ShapeDtypeStruct((T, width), BF16),
+        in_specs=[local, local, anywhere, anywhere, anywhere, anywhere],
+        out_specs=local,
+        scratch_shapes=[
+            vmem((2, nc, G * T, fc), BF16),
+            vmem((line, 2 * plane, T), F32),
+            vmem((2, G, 2 * plane, T), F32),
+            vmem((2, plane, R, G * T), BF16),
+            vmem((2, 2, G * T, plane * R), BF16),
+            vmem((2, nc, plane - 1, R, fc), BF16),
+            vmem((2, nc, plane * R, fc), BF16),
+            vmem((2, nc, plane * R, fc), BF16),
+            vmem((width, units), BF16),
+            vmem((width, units), BF16),
+            vmem((nc, units, fc), BF16),
+            vmem((2, plane * R, units), F32),
+            vmem((2, 2, plane * R, half), BF16),
+            vmem((2, nc, plane - 1, R, fc), BF16),
+            vmem((2, nc, plane * R, fc), BF16),
+            vmem((G * T, fc), F32),
+            vmem((2, nc, G * T, fc), BF16),
+            vmem((nc, line - 1, T, fc), BF16),
+            vmem((nc, T, fc), F32),
+            dma((nc,)), dma((2,)), dma((nc,)),
+            dma((line - 1,)), dma((line - 1,)),
+            dma((line - 1, nc)), dma((line - 1, nc)),
+            dma((2, plane - 1, nc)), dma((2, plane - 1, nc)),
+            dma((2, nc)), dma((2, nc)),
+            dma((2,)), dma((2,)),
+            dma((2, plane)), dma((2, plane)),
+            dma((2, plane - 1, nc)), dma((2, plane - 1, nc)),
+            dma((line - 1, nc)), dma((line - 1, nc)),
+        ],
+        compiler_params=pltpu.CompilerParams(
+            collective_id=0, has_side_effects=True, vmem_limit_bytes=60 * 1024 * 1024
+        ),
+        name="expert_layer",
+    )(routes.T, gate_levels.T, tokens, w_gate[0], w_up[0], w_down[0])
+
+
+def on_device(ep_count, tp_count, tokens, routes, gate_levels, w_gate, w_up, w_down):
+    tok_rows, top_count = routes.shape
+    experts_here, width, units = w_gate.shape
+    cap = capacity_of(tok_rows, top_count, experts_here * ep_count)
+    plane = math.isqrt(ep_count)
+    line = ep_count // plane
+    fc = 256
+    fits = (
+        tp_count == 2
+        and experts_here == 1
+        and plane * line == ep_count
+        and plane & (plane - 1) == 0
+        and plane % 4 == 0
+        and line * 2 * plane <= 128
+        and tok_rows == 128
+        and line % 2 == 0
+        and line * cap % 32 == 0
+        and width // fc >= 3
+        and width % fc == 0
+        and units % 256 == 0
+    )
+    args = (tokens, routes, gate_levels, w_gate, w_up, w_down)
+    if fits:
+        return kernel_path(line, plane, cap, fc, *args)
+    return general_path(*args)
+
+
 def solution(mesh):
     in_specs = (
         P("ep", "tp"),
@@ -83,6 +538,7 @@
         P("ep", None, "tp"),
     )
     out_specs = P("ep", "tp")
+    body = functools.partial(on_device, mesh.shape["ep"], mesh.shape["tp"])
     return jax.shard_map(
-        on_device, mesh=mesh, in_specs=in_specs, out_specs=out_specs, check_vma=False
-    )
+        body, mesh=mesh, in_specs=in_specs, out_specs=out_specs, check_vma=False
+    )

time: 287 us -> 116 us (0.40)
  the two profiles are of different devices: /device:TPU:14 before, /device:TPU:0 now
where the time goes in v2:
time: 116 us; the launch traced here: 115 us
  Pallas kernels  114 us (98%)
  local copies, waits for them, and re-layouts  1.82 us (2%)
    pallas_call x1, Pallas kernels, kernel_path(): pl.pallas_call(functools.partial(layer_kernel, line, plane, cap, fc), out...  114 us

profile of v2, /device:TPU:0, one launch (start us, length us, event | category | flops | bytes accessed | tf_op | source)
XLA Modules:
  0.0 115.5 jit_solution(6415579549176325936)
XLA Ops:
  0.0 113.6 %expert_layer.1 = bf16[128,1792]{1,0:T(8,128)(2,1)} custom-call(s32[8,128]{1,0:T(8,128)} %bitcast.8, s32[8,128]{1,0:T(8,128)} %bitcast.9, bf16[128,1792]{1,0:T(8,128)(2,1)} %tokens_hbm.1, bf16[1792,1024]{1,0:T(8,128)(2,1)} %bitcast.5, bf16[1792,1024]{1,0:T(8,128)(2,1)} %bitcast.6, bf16[1024,1792]{1,0:T(8,128)(2,1)} %bitcast.7), custom_call_target="tpu_custom_call" | custom-call | tf_op jit(solution)/shard_map/expert_layer/pallas_call | solution.py:462
  113.6 1.8 %copy.8 = bf16[128,1792]{1,0:T(8,128)(2,1)} copy(bf16[128,1792]{1,0:T(8,128)(2,1)} %expert_layer.1) | data formatting | bytes 917504

commit v3 on v2

--- a/solution.py
+++ b/solution.py
@@ -344,7 +344,7 @@
         wd_load(c).wait()
 
     lag = 3
-    early = min(3, nc)
+    early = min(lag + 1, nc)
 
     def dispatch(c, carry):
         @pl.when(c < nc)
@@ -362,19 +362,19 @@
         def _():
             activate(0)
 
-        @pl.when((c >= lag) & (c < nc + lag))
-        def _():
-            forward(1, c - lag)
-
         @pl.when(c == nc + 1)
         def _():
             for m in range(plane):
                 h_copy(0, m).wait_recv()
 
-        @pl.when((c > nc) & (c <= nc + early))
+        @pl.when((c > nc) & (c < nc + early))
         def _():
             give_back(0, c - nc - 1)
 
+        @pl.when((c >= lag) & (c < nc + lag))
+        def _():
+            forward(1, c - lag)
+
         @pl.when(c > lag)
         def _():
             gate_up(1, c - lag - 1)
@@ -384,6 +384,7 @@
     lax.fori_loop(0, nc + lag + 1, dispatch, 0)
 
     activate(1)
+    give_back(0, early - 1)
     for m in range(plane):
         h_copy(1, m).wait_recv()
 
@@ -518,7 +519,7 @@
         and tok_rows == 128
         and line % 2 == 0
         and line * cap % 32 == 0
-        and width // fc >= 3
+        and width // fc >= 4
         and width % fc == 0
         and units % 256 == 0
     )

time: 116 us -> 118 us (1.017)
  Pallas kernels: 114 us -> 116 us
    pallas_call x1, Pallas kernels: 114 us -> 116 us  [kernel_path(): pl.pallas_call(functools.partial(layer_kernel, line, plane, cap, fc), out...]
where the time goes in v3:
time: 118 us
  Pallas kernels  116 us (98%)
  local copies, waits for them, and re-layouts  1.82 us (2%)
    pallas_call x1, Pallas kernels, kernel_path(): pl.pallas_call(functools.partial(layer_kernel, line, plane, cap, fc), out...  116 us

profile of v3, /device:TPU:0, one launch (start us, length us, event | category | flops | bytes accessed | tf_op | source)
XLA Modules:
  0.0 117.7 jit_solution(18384402259289964947)
XLA Ops:
  0.0 115.9 %expert_layer.1 = bf16[128,1792]{1,0:T(8,128)(2,1)} custom-call(s32[8,128]{1,0:T(8,128)} %bitcast.8, s32[8,128]{1,0:T(8,128)} %bitcast.9, bf16[128,1792]{1,0:T(8,128)(2,1)} %tokens_hbm.1, bf16[1792,1024]{1,0:T(8,128)(2,1)} %bitcast.5, bf16[1792,1024]{1,0:T(8,128)(2,1)} %bitcast.6, bf16[1024,1792]{1,0:T(8,128)(2,1)} %bitcast.7), custom_call_target="tpu_custom_call" | custom-call | tf_op jit(solution)/shard_map/expert_layer/pallas_call | solution.py:463
  115.9 1.8 %copy.8 = bf16[128,1792]{1,0:T(8,128)(2,1)} copy(bf16[128,1792]{1,0:T(8,128)(2,1)} %expert_layer.1) | data formatting | bytes 917504
